TPU v7x, 32 devices: a whole 2x2x4 slice. The times are simulated.
32 devices in a mesh: gx: 2 (over x), gy: 4 (over y, core), gz: 4 (over z).
Axes of the slice: x: 2, y: 2, z: 4, core: 2. Of those that a mesh axis runs over, the one named last changes fastest.
Arguments:
- blocks: bfloat16 [512, 128, 1024], P(('gx', 'gy', 'gz')), may hold values from -0.375 to 0.375
- counts: int32 [512], P(('gx', 'gy', 'gz')), may hold values from 1 to 128
- owner: int32 [512, 1], P(('gx', 'gy', 'gz')), may hold values from 0 to 15; in each aligned block of 16 rows (0 to 15, 16 to 31, ...) no two rows name the same one
- kdiag: float32 [32, 1024], P(('gx', 'gy', 'gz')), may hold values from 0.5 to 4
- rhs: float32 [32, 1024], P(('gx', 'gy', 'gz')), may hold values from -40 to 40
- modes: float32 [32, 6, 1024], P(('gx', 'gy', 'gz')), may hold values from -6 to 6
Outputs:
- schur: bfloat16 [32, 1024, 1024], P(('gx', 'gy', 'gz'))
- solution: float32 [32, 1024], P(('gx', 'gy', 'gz'))
- residual: float32 [32, 1024], P(('gx', 'gy', 'gz'))
Inputs may be any that keep to these rules, and one draw needn't show every extreme that they name: `owner`: the 16 blocks of one device go to different owners.
All inputs are finite; a program needn't handle non-finite values.
Results may differ from a plain program's by a relative error of at most 0.001.
Values may be sent and summed in bfloat16 or wider, within the bound.
A program may use at most 64 MiB of HBM per device.

v0:
```python
import jax
import jax.numpy as jnp
from jax import lax
from jax.sharding import PartitionSpec as P

ITERS = 2


def extended(block, sides, width):
    for axis, dim in sides:
        count = lax.axis_size(axis)
        forward = [(i, i + 1) for i in range(count - 1)]
        forward.append((count - 1, 0))
        backward = [(target, source) for source, target in forward]
        low = lax.ppermute(
            lax.slice_in_dim(block, block.shape[dim] - width, None, axis=dim), axis, forward
        )
        high = lax.ppermute(lax.slice_in_dim(block, 0, width, axis=dim), axis, backward)
        block = jnp.concatenate([low, block, high], axis=dim)
    return block


def add_faces(values, grid):
    width = values.shape[1]
    face = width // 8
    extra = jnp.concatenate(
        [
            grid[2, 1, 1][:, face : 2 * face],
            grid[0, 1, 1][:, 0:face],
            grid[1, 2, 1][:, 3 * face : 4 * face],
            grid[1, 0, 1][:, 2 * face : 3 * face],
            grid[1, 1, 2][:, 6 * face : 8 * face],
            grid[1, 1, 0][:, 4 * face : 6 * face],
        ],
        axis=1,
    )
    return values + extra


def shards(blocks, counts, owner, kdiag, rhs, modes):
    hi = lax.Precision.HIGHEST
    nblk, nrows, width = blocks.shape
    size_y = lax.axis_size("gy")
    size_z = lax.axis_size("gz")
    owners = size_y * size_z
    rowid = lax.broadcasted_iota(jnp.int32, (nblk, nrows, 1), 1)
    masked = jnp.where(rowid < counts[:, None, None], blocks, jnp.zeros_like(blocks))
    target = lax.broadcasted_iota(jnp.int32, (owners, nblk), 0)
    pick = (owner[:, 0][None, :] == target).astype(jnp.bfloat16)
    outgoing = jnp.dot(
        pick, masked.reshape(nblk, nrows * width), preferred_element_type=jnp.bfloat16
    )
    outgoing = outgoing.reshape(owners, nrows, width)
    arrived = lax.all_to_all(outgoing, ("gy", "gz"), split_axis=0, concat_axis=0, tiled=True)
    flat = arrived.reshape(owners * nrows, width)
    gram = lax.dot_general(flat, flat, (((0,), (0,)), ((), ())), preferred_element_type=jnp.float32)
    stiff = gram + jnp.diag(kdiag[0])
    schur = stiff.astype(jnp.bfloat16)[None]
    stacked = jnp.concatenate([rhs, modes[0]], axis=0)
    grid = extended(stacked[None, None, None], (("gx", 0), ("gy", 1), ("gz", 2)), 1)
    loaded = add_faces(stacked, grid)
    force = loaded[0]
    basis = loaded[1:]
    coarse, gforce, fnorm = lax.psum(
        (
            0.5 * jnp.dot(basis, basis.T, precision=hi),
            0.5 * jnp.dot(basis, force, precision=hi),
            0.5 * jnp.sum(force * force),
        ),
        ("gx", "gy", "gz"),
    )
    factor = jnp.linalg.cholesky(coarse)
    coef = jax.scipy.linalg.cho_solve((factor, True), gforce)
    residual = force - jnp.dot(coef, basis, precision=hi)
    norm_now = fnorm - jnp.dot(gforce, coef, precision=hi)
    direction = residual
    solution = jnp.zeros_like(force)
    for step in range(ITERS):
        local = jnp.dot(stiff, direction, precision=hi)
        faces = extended(local[None, None, None, None], (("gx", 0), ("gy", 1), ("gz", 2)), 1)
        image = add_faces(local[None], faces)[0]
        gimage, curve, square, cross = lax.psum(
            (
                0.5 * jnp.dot(basis, image, precision=hi),
                0.5 * jnp.sum(direction * image),
                0.5 * jnp.sum(image * image),
                0.5 * jnp.sum(residual * image),
            ),
            ("gx", "gy", "gz"),
        )
        coef = jax.scipy.linalg.cho_solve((factor, True), gimage)
        along = image - jnp.dot(coef, basis, precision=hi)
        alpha = norm_now / curve
        along_sq = (
            square
            - 2.0 * jnp.dot(coef, gimage, precision=hi)
            + jnp.dot(coef, jnp.dot(coarse, coef, precision=hi), precision=hi)
        )
        norm_next = norm_now - 2.0 * alpha * cross + alpha * alpha * along_sq
        solution = solution + alpha * direction
        residual = residual - alpha * along
        direction = residual + norm_next / norm_now * direction
        norm_now = norm_next
    return (schur, solution[None], residual[None])


def solution(mesh):
    in_specs = (
        P(("gx", "gy", "gz"), None, None),
        P(("gx", "gy", "gz")),
        P(("gx", "gy", "gz"), None),
        P(("gx", "gy", "gz"), None),
        P(("gx", "gy", "gz"), None),
        P(("gx", "gy", "gz"), None, None),
    )
    out_specs = (
        P(("gx", "gy", "gz"), None, None),
        P(("gx", "gy", "gz"), None),
        P(("gx", "gy", "gz"), None),
    )
    return jax.shard_map(shards, mesh=mesh, in_specs=in_specs, out_specs=out_specs, check_vma=False)
```

profile of v0, /device:TPU:12, one launch (start us, length us, event | category | flops | bytes accessed | tf_op | source)
XLA Modules:
  0.0 312.4 jit_solution(2874678932765971015)
XLA Ops:
  0.6 0.7 iota_compare_fusion.1
  1.4 2.5 broadcast_select_fusion
  3.9 3.0 fusion
  6.8 4.3 %copy.15 = bf16[16,128,1024]{2,1,0:T(8,128)(2,1)} copy(bf16[16,128,1024]{2,0,1:T(8,128)(2,1)S(1)} %fusion) | data formatting | bytes 8388608 | tf_op jit(solution)/shard_map/dot_general | solution.py:50
  11.1 6.4 %all-to-all-start = ((bf16[16,128,1024]{2,1,0:T(8,128)(2,1)}), bf16[16,128,1024]{2,1,0:T(8,128)(2,1)}, u32[]{:S(2)}, u32[]{:S(2)}) async-start(bf16[16,128,1024]{2,1,0:T(8,128)(2,1)} %copy.15), calls=%async_computation | async-start | bytes 8388608 | tf_op jit(solution)/shard_map/all_to_all | solution.py:54
  17.6 1.6 collective-permute-start
  19.1 0.5 collective-permute-start.1
  19.7 1.9 collective-permute-done
  21.5 1.5 collective-permute-done.1
  23.1 0.5 collective-permute-start.3
  23.6 16.4 %collective-permute-done.2 = f32[3,1,1,7,1024]{4,3,2,1,0:T(8,128)S(1)} collective-permute-done((f32[3,1,1,7,1024]{4,3,2,1,0:T(8,128)S(1)}, f32[3,1,1,7,1024]{4,3,2,1,0:T(8,128)S(1)}, u32[]{:S(2)}, u32[]{:S(2)}) %collective-permute-start.2) | collective-permute-done | bytes 86048 | tf_op jit(solution)/shard_map/ppermute | solution.py:18
  40.5 19.8 %collective-permute-start.4 = (f32[3,3,1,7,1024]{4,3,2,1,0:T(8,128)S(1)}, f32[3,3,1,7,1024]{4,3,2,1,0:T(8,128)S(1)}, u32[]{:S(2)}, u32[]{:S(2)}) collective-permute-start(f32[3,3,1,7,1024]{4,3,2,1,0:T(8,128)S(1)} %pad_maximum_fusion), channel_id=1, source_target_pairs={{1,0},{2,1},{3,2},{0,3},{5,4},{6,5},{7,6},{4,7},{9,8},{10,9},{11,1... | collective-permute-start | bytes 774152 | tf_op jit(solution)/shard_map/ppermute | solution.py:18
  60.3 62.5 %collective-permute-done.4 = f32[3,3,1,7,1024]{4,3,2,1,0:T(8,128)S(1)} collective-permute-done((f32[3,3,1,7,1024]{4,3,2,1,0:T(8,128)S(1)}, f32[3,3,1,7,1024]{4,3,2,1,0:T(8,128)S(1)}, u32[]{:S(2)}, u32[]{:S(2)}) %collective-permute-start.4) | collective-permute-done | bytes 258080 | tf_op jit(solution)/shard_map/ppermute | solution.py:18
  123.1 39.6 %all-reduce.2 = (f32[6,6]{1,0:T(8,128)S(1)}, f32[6]{0:T(128)S(1)}) all-reduce(f32[6,6]{1,0:T(8,128)S(1)} %convolution_multiply_fusion, f32[6]{0:T(128)S(1)} %fusion.13), channel_id=1, replica_groups=mesh['gx'=2,'gy'=4,'gz'=4] {'gx','gy','gz'}, use_global_device_ids=true, to_apply=%region_3.4 | all-reduce | flops 42 | bytes 336 | tf_op jit(solution)/shard_map/psum | solution.py:64
  162.8 0.5 cholesky.18
  163.3 0.6 compare_reduce_fusion
  164.0 0.6 fusion.30
  165.2 0.8 fusion.48
  166.2 0.6 multiply_reduce_fusion.3
  166.8 7.6 %fusion.53 = f32[1024,1024,1]{1,0,2:T(8,128)S(1)} fusion(bf16[16,128,1024]{2,1,0:T(8,128)(2,1)} %all-to-all-done), kind=kOutput, calls=%fused_computation.129 | convolution fusion | flops 4294967296 | bytes 8388608 | tf_op jit(solution)/shard_map/dot_general | solution.py:56
  174.4 1.9 copy-done
  176.3 3.7 %fusion.4 = f32[1,1024]{1,0:T(1,128)S(1)} fusion(f32[1024,1]{0,1:T(1,128)S(1)} %bitcast.222, f32[1024,1024,1]{1,0,2:T(8,128)S(1)} %fusion.53, f32[1024]{0:T(1024)S(1)} %bitcast.238), kind=kOutput, calls=%fused_computation.7 | convolution fusion | flops 15728640 | bytes 4206592 | tf_op jit(solution)/shard_map/dot_general | solution.py:79
  180.0 0.6 collective-permute-start.6
  180.6 1.5 collective-permute-start.7
  182.7 0.9 collective-permute-done.6
  183.6 0.6 collective-permute-done.7
  184.8 0.9 collective-permute-done.8
  185.7 1.9 collective-permute-done.9
  187.6 2.1 collective-permute-start.10
  189.8 1.8 collective-permute-done.10
  191.6 2.1 collective-permute-done.11
  193.7 0.6 multiply_reduce_fusion.1
  195.8 42.9 %all-reduce.1 = (f32[]{:T(128)}, f32[]{:T(128)}, f32[]{:T(128)}, f32[6]{0:T(128)S(1)}) all-reduce(f32[]{:T(128)S(6)} %mul.83, f32[]{:T(128)S(6)} %mul.88, f32[]{:T(128)S(6)} %mul.95, f32[6]{0:T(128)S(1)} %fusion.12), channel_id=1, replica_groups=mesh['gx'=2,'gy'=4,'gz'=4] {'gx','gy','gz'}, use_global_device_ids=true, to_apply=%region_1.2 | all-reduce | flops 9 | bytes 72 | tf_op jit(solution)/shard_map/psum | solution.py:64
  238.8 0.8 fusion.45
  239.6 0.8 fusion.15
  245.2 5.9 %fusion.3 = f32[1,1024]{1,0:T(1,128)S(1)} fusion(f32[1024,1]{0,1:T(1,128)S(1)} %bitcast.223, f32[1024,1024,1]{1,0,2:T(8,128)} %copy-done, f32[1024]{0:T(1024)S(1)} %bitcast.239), kind=kOutput, calls=%fused_computation.6 | convolution fusion | flops 15728640 | bytes 4206592 | tf_op jit(solution)/shard_map/dot_general | solution.py:79
  251.0 0.7 collective-permute-start.12
  251.7 1.4 collective-permute-start.13
  253.1 1.6 collective-permute-done.12
  254.6 0.7 collective-permute-done.13
  255.9 0.9 collective-permute-done.14
  256.8 1.8 collective-permute-done.15
  258.7 2.0 collective-permute-start.17
  260.7 2.3 collective-permute-done.16
  263.1 0.6 multiply_reduce_fusion
  264.5 4.0 %fusion.6 = bf16[1,1024,1024]{2,1,0:T(8,128)(2,1)} fusion(f32[1024,1024,1]{1,0,2:T(8,128)} %copy-done, f32[1024]{0:T(1024)S(1)} %bitcast.240), kind=kLoop, calls=%fused_computation.9 | loop fusion | flops 4194304 | bytes 6295552 | tf_op jit(solution)/shard_map/broadcast_in_dim | solution.py:58
  268.4 42.2 %all-reduce = (f32[]{:T(128)}, f32[6]{0:T(128)S(1)}) all-reduce(f32[]{:T(128)S(6)} %mul.103, f32[6]{0:T(128)S(1)} %fusion.11), channel_id=1, replica_groups=mesh['gx'=2,'gy'=4,'gz'=4] {'gx','gy','gz'}, use_global_device_ids=true, to_apply=%region_12.14 | all-reduce | flops 7 | bytes 56 | tf_op jit(solution)/shard_map/psum | solution.py:82
  311.8 0.6 multiply_subtract_fusion
  (83 shorter events, 4.3 us)
Async XLA Ops:
  1.4 2.5 copy-start.4
  11.1 6.4 %copy-start.2 = (f32[1,6,1024]{2,0,1:T(1,128)S(1)}, f32[1,6,1024]{2,0,1:T(1,128)}, u32[]{:S(2)}) copy-start(f32[1,6,1024]{2,0,1:T(1,128)} %param.13) | copy-start | bytes 73732
  11.1 6.4 %copy-start.3 = (f32[1,1024]{1,0:T(1,128)S(1)}, f32[1,1024]{1,0:T(1,128)}, u32[]{:S(2)}) copy-start(f32[1,1024]{1,0:T(1,128)} %param.12) | copy-start | bytes 12292
  11.1 155.6 %all-to-all-start = ((bf16[16,128,1024]{2,1,0:T(8,128)(2,1)}), bf16[16,128,1024]{2,1,0:T(8,128)(2,1)}, u32[]{:S(2)}, u32[]{:S(2)}) async-start(bf16[16,128,1024]{2,1,0:T(8,128)(2,1)} %copy.15), calls=%async_computation | async-start | bytes 8388608 | tf_op jit(solution)/shard_map/all_to_all | solution.py:54
  17.6 4.0 %collective-permute-start = (f32[1,1,1,7,1024]{4,3,2,1,0:T(8,128)S(1)}, f32[1,1,1,7,1024]{4,3,2,1,0:T(8,128)S(1)}, u32[]{:S(2)}, u32[]{:S(2)}) collective-permute-start(f32[1,1,1,7,1024]{4,3,2,1,0:T(8,128)S(1)} %fusion.17), channel_id=1, source_target_pairs={{16,0},{0,16},{17,1},{1,17},{18,2},{2,18},{19,3},{3,19},{20,4},{4,... | collective-permute-start | bytes 86024 | tf_op jit(solution)/shard_map/ppermute | solution.py:18
  19.1 3.9 %collective-permute-start.1 = (f32[1,1,1,7,1024]{4,3,2,1,0:T(8,128)S(1)}, f32[1,1,1,7,1024]{4,3,2,1,0:T(8,128)S(1)}, u32[]{:S(2)}, u32[]{:S(2)}) collective-permute-start(f32[1,1,1,7,1024]{4,3,2,1,0:T(8,128)S(1)} %fusion.17), channel_id=1, source_target_pairs={{0,16},{16,0},{1,17},{17,1},{2,18},{18,2},{3,19},{19,3},{4,20},{20... | collective-permute-start | bytes 86024 | tf_op jit(solution)/shard_map/ppermute | solution.py:15
  23.1 16.9 %collective-permute-start.2 = (f32[3,1,1,7,1024]{4,3,2,1,0:T(8,128)S(1)}, f32[3,1,1,7,1024]{4,3,2,1,0:T(8,128)S(1)}, u32[]{:S(2)}, u32[]{:S(2)}) collective-permute-start(f32[3,1,1,7,1024]{4,3,2,1,0:T(8,128)S(1)} %pad_maximum_fusion.1), channel_id=1, source_target_pairs={{4,0},{8,4},{12,8},{0,12},{5,1},{9,5},{13,9},{1,13},{6,2},{10,6},{... | collective-permute-start | bytes 258056 | tf_op jit(solution)/shard_map/ppermute | solution.py:18
  23.1 17.3 %collective-permute-start.3 = (f32[3,1,1,7,1024]{4,3,2,1,0:T(8,128)S(1)}, f32[3,1,1,7,1024]{4,3,2,1,0:T(8,128)S(1)}, u32[]{:S(2)}, u32[]{:S(2)}) collective-permute-start(f32[3,1,1,7,1024]{4,3,2,1,0:T(8,128)S(1)} %pad_maximum_fusion.1), channel_id=1, source_target_pairs={{0,4},{4,8},{8,12},{12,0},{1,5},{5,9},{9,13},{13,1},{2,6},{6,10},{... | collective-permute-start | bytes 258056 | tf_op jit(solution)/shard_map/ppermute | solution.py:15
  40.5 82.2 %collective-permute-start.4 = (f32[3,3,1,7,1024]{4,3,2,1,0:T(8,128)S(1)}, f32[3,3,1,7,1024]{4,3,2,1,0:T(8,128)S(1)}, u32[]{:S(2)}, u32[]{:S(2)}) collective-permute-start(f32[3,3,1,7,1024]{4,3,2,1,0:T(8,128)S(1)} %pad_maximum_fusion), channel_id=1, source_target_pairs={{1,0},{2,1},{3,2},{0,3},{5,4},{6,5},{7,6},{4,7},{9,8},{10,9},{11,1... | collective-permute-start | bytes 774152 | tf_op jit(solution)/shard_map/ppermute | solution.py:18
  60.2 62.5 %collective-permute-start.5 = (f32[3,3,1,7,1024]{4,3,2,1,0:T(8,128)S(1)}, f32[3,3,1,7,1024]{4,3,2,1,0:T(8,128)S(1)}, u32[]{:S(2)}, u32[]{:S(2)}) collective-permute-start(f32[3,3,1,7,1024]{4,3,2,1,0:T(8,128)S(1)} %pad_maximum_fusion), channel_id=1, source_target_pairs={{0,1},{1,2},{2,3},{3,0},{4,5},{5,6},{6,7},{7,4},{8,9},{9,10},{10,1... | collective-permute-start | bytes 774152 | tf_op jit(solution)/shard_map/ppermute | solution.py:15
  166.8 9.5 %copy-start.1 = (f32[1,1024]{1,0:T(1,128)S(1)}, f32[1,1024]{1,0:T(1,128)}, u32[]{:S(2)}) copy-start(f32[1,1024]{1,0:T(1,128)} %param.11) | copy-start | bytes 12292
  174.4 1.9 copy-start
  180.0 3.6 %collective-permute-start.6 = (f32[1,1,1,1,1024]{4,3,2,1,0:T(1,128)S(1)}, f32[1,1,1,1,1024]{4,3,2,1,0:T(1,128)S(1)}, u32[]{:S(2)}, u32[]{:S(2)}) collective-permute-start(f32[1,1,1,1,1024]{4,3,2,1,0:T(1,128)S(1)} %bitcast.224), channel_id=1, source_target_pairs={{16,0},{0,16},{17,1},{1,17},{18,2},{2,18},{19,3},{3,19},{20,4},{4,... | collective-permute-start | bytes 12296 | tf_op jit(solution)/shard_map/ppermute | solution.py:18
  180.6 3.6 %collective-permute-start.7 = (f32[1,1,1,1,1024]{4,3,2,1,0:T(1,128)S(1)}, f32[1,1,1,1,1024]{4,3,2,1,0:T(1,128)S(1)}, u32[]{:S(2)}, u32[]{:S(2)}) collective-permute-start(f32[1,1,1,1,1024]{4,3,2,1,0:T(1,128)S(1)} %bitcast.225), channel_id=1, source_target_pairs={{0,16},{16,0},{1,17},{17,1},{2,18},{18,2},{3,19},{19,3},{4,20},{20... | collective-permute-start | bytes 12296 | tf_op jit(solution)/shard_map/ppermute | solution.py:15
  184.2 1.5 collective-permute-start.8
  184.3 3.3 %collective-permute-start.9 = (f32[3,1,1,1,1024]{4,3,2,1,0:T(1,128)S(1)}, f32[3,1,1,1,1024]{4,3,2,1,0:T(1,128)S(1)}, u32[]{:S(2)}, u32[]{:S(2)}) collective-permute-start(f32[3,1,1,1,1024]{4,3,2,1,0:T(1,128)S(1)} %pad_maximum_fusion.5), channel_id=1, source_target_pairs={{0,4},{4,8},{8,12},{12,0},{1,5},{5,9},{9,13},{13,1},{2,6},{6,10},{... | collective-permute-start | bytes 36872 | tf_op jit(solution)/shard_map/ppermute | solution.py:15
  187.6 4.0 %collective-permute-start.10 = (f32[3,3,1,1,1024]{4,3,2,1,0:T(1,128)S(1)}, f32[3,3,1,1,1024]{4,3,2,1,0:T(1,128)S(1)}, u32[]{:S(2)}, u32[]{:S(2)}) collective-permute-start(f32[3,3,1,1,1024]{4,3,2,1,0:T(1,128)S(1)} %pad_maximum_fusion.2), channel_id=1, source_target_pairs={{1,0},{2,1},{3,2},{0,3},{5,4},{6,5},{7,6},{4,7},{9,8},{10,9},{11,1... | collective-permute-start | bytes 110600 | tf_op jit(solution)/shard_map/ppermute | solution.py:18
  189.7 4.0 %collective-permute-start.11 = (f32[3,3,1,1,1024]{4,3,2,1,0:T(1,128)S(1)}, f32[3,3,1,1,1024]{4,3,2,1,0:T(1,128)S(1)}, u32[]{:S(2)}, u32[]{:S(2)}) collective-permute-start(f32[3,3,1,1,1024]{4,3,2,1,0:T(1,128)S(1)} %pad_maximum_fusion.2), channel_id=1, source_target_pairs={{0,1},{1,2},{2,3},{3,0},{4,5},{5,6},{6,7},{7,4},{8,9},{9,10},{10,1... | collective-permute-start | bytes 110600 | tf_op jit(solution)/shard_map/ppermute | solution.py:15
  251.0 3.6 %collective-permute-start.12 = (f32[1,1,1,1,1024]{4,3,2,1,0:T(1,128)S(1)}, f32[1,1,1,1,1024]{4,3,2,1,0:T(1,128)S(1)}, u32[]{:S(2)}, u32[]{:S(2)}) collective-permute-start(f32[1,1,1,1,1024]{4,3,2,1,0:T(1,128)S(1)} %bitcast.229), channel_id=1, source_target_pairs={{16,0},{0,16},{17,1},{1,17},{18,2},{2,18},{19,3},{3,19},{20,4},{4,... | collective-permute-start | bytes 12296 | tf_op jit(solution)/shard_map/ppermute | solution.py:18
  251.7 3.6 %collective-permute-start.13 = (f32[1,1,1,1,1024]{4,3,2,1,0:T(1,128)S(1)}, f32[1,1,1,1,1024]{4,3,2,1,0:T(1,128)S(1)}, u32[]{:S(2)}, u32[]{:S(2)}) collective-permute-start(f32[1,1,1,1,1024]{4,3,2,1,0:T(1,128)S(1)} %bitcast.230), channel_id=1, source_target_pairs={{0,16},{16,0},{1,17},{17,1},{2,18},{18,2},{3,19},{19,3},{4,20},{20... | collective-permute-start | bytes 12296 | tf_op jit(solution)/shard_map/ppermute | solution.py:15
  255.3 1.5 collective-permute-start.14
  255.4 3.2 %collective-permute-start.15 = (f32[3,1,1,1,1024]{4,3,2,1,0:T(1,128)S(1)}, f32[3,1,1,1,1024]{4,3,2,1,0:T(1,128)S(1)}, u32[]{:S(2)}, u32[]{:S(2)}) collective-permute-start(f32[3,1,1,1,1024]{4,3,2,1,0:T(1,128)S(1)} %pad_maximum_fusion.6), channel_id=1, source_target_pairs={{0,4},{4,8},{8,12},{12,0},{1,5},{5,9},{9,13},{13,1},{2,6},{6,10},{... | collective-permute-start | bytes 36872 | tf_op jit(solution)/shard_map/ppermute | solution.py:15
  258.6 4.4 %collective-permute-start.16 = (f32[3,3,1,1,1024]{4,3,2,1,0:T(1,128)S(1)}, f32[3,3,1,1,1024]{4,3,2,1,0:T(1,128)S(1)}, u32[]{:S(2)}, u32[]{:S(2)}) collective-permute-start(f32[3,3,1,1,1024]{4,3,2,1,0:T(1,128)S(1)} %pad_maximum_fusion.3), channel_id=1, source_target_pairs={{1,0},{2,1},{3,2},{0,3},{5,4},{6,5},{7,6},{4,7},{9,8},{10,9},{11,1... | collective-permute-start | bytes 110600 | tf_op jit(solution)/shard_map/ppermute | solution.py:18
  258.7 4.4 %collective-permute-start.17 = (f32[3,3,1,1,1024]{4,3,2,1,0:T(1,128)S(1)}, f32[3,3,1,1,1024]{4,3,2,1,0:T(1,128)S(1)}, u32[]{:S(2)}, u32[]{:S(2)}) collective-permute-start(f32[3,3,1,1,1024]{4,3,2,1,0:T(1,128)S(1)} %pad_maximum_fusion.3), channel_id=1, source_target_pairs={{0,1},{1,2},{2,3},{3,0},{4,5},{5,6},{6,7},{7,4},{8,9},{9,10},{10,1... | collective-permute-start | bytes 110600 | tf_op jit(solution)/shard_map/ppermute | solution.py:15
where the time goes:
time: 313 us; the launch traced here: 312 us
  blocking collectives  125 us (40%)
  waiting for transfers between devices  98 us (31%)
  starting transfers between devices  38.2 us (12%)
  matrix products  24.1 us (8%)
  other arithmetic  12.1 us (4%)
  between operations  8.84 us (3%)
  local copies, waits for them, and re-layouts  6.48 us (2%)
    ppermute x9, waiting for transfers between devices, extended(): lax.ppermute(lax.slice_in_dim(block, 0, width, axis=dim), axis, backward)  89.1 us
    psum x2, blocking collectives, shards(): lax.psum((0.5 * jnp.dot(basis, basis.T, precision=hi), 0.5 * jnp.dot(basi...  82.4 us
    psum x1, blocking collectives, shards(): lax.psum((0.5 * jnp.dot(basis, image, precision=hi), 0.5 * jnp.sum(direct...  42.2 us
    ppermute x9, starting transfers between devices, extended(): lax.ppermute(lax.slice_in_dim(block, 0, width, axis=dim), axis, backward)  25 us
    dot_general x2, matrix products, shards(): local = jnp.dot(stiff, direction, precision=hi)  9.54 us
    ppermute x9, waiting for transfers between devices, extended(): lax.ppermute(lax.slice_in_dim(block, block.shape[dim] - width, None, axis...  8.88 us
    dot_general x1, matrix products, shards(): lax.dot_general(flat, flat, (((0,), (0,)), ((), ())), preferred_element_t...  7.58 us
    ppermute x9, starting transfers between devices, extended(): lax.ppermute(lax.slice_in_dim(block, block.shape[dim] - width, None, axis...  6.87 us
  transfers between devices with their start and end apart: 19, of which 16 were waited for; matrix products, arithmetic and copies ran while one was open for 1% of the time, Pallas kernels for 0%

commit v1 on v0

--- a/solution.py
+++ b/solution.py
@@ -79,14 +79,20 @@
         local = jnp.dot(stiff, direction, precision=hi)
         faces = extended(local[None, None, None, None], (("gx", 0), ("gy", 1), ("gz", 2)), 1)
         image = add_faces(local[None], faces)[0]
-        gimage, curve, square, cross = lax.psum(
+
+        def handle_the_steps_all(arr_in, device_axis, named_axis):
+            before = lax.psum(arr_in, device_axis)
+            return lax.psum(before, axis_name=named_axis)
+
+        gimage, curve, square, cross = handle_the_steps_all(
             (
                 0.5 * jnp.dot(basis, image, precision=hi),
                 0.5 * jnp.sum(direction * image),
                 0.5 * jnp.sum(image * image),
                 0.5 * jnp.sum(residual * image),
             ),
-            ("gx", "gy", "gz"),
+            ("gy", "gz"),
+            "gx",
         )
         coef = jax.scipy.linalg.cho_solve((factor, True), gimage)
         along = image - jnp.dot(coef, basis, precision=hi)

time: 313 us -> 308 us (0.984)
  blocking collectives: 125 us -> 118 us
    psum x2 -> x1, blocking collectives: 82.4 us -> 39.9 us  [shards(): lax.psum((0.5 * jnp.dot(basis, basis.T, precision=hi), 0.5 * jnp.dot(basi...]
    psum x1 -> x4, blocking collectives: 42.2 us -> 78 us  [the longest x2 67 us: handle_the_steps_all(): before = lax.psum(arr_in, device_axis)]
  transfers between devices with their start and end apart: 19 -> 19, of which waited for: 16 -> 17; matrix products, arithmetic and copies ran while one was open for 1% -> 1% of each run, Pallas kernels for 0% -> 0%
where the time goes in v1:
time: 308 us; the launch traced here: 307 us
  blocking collectives  118 us (38%)
  waiting for transfers between devices  99 us (32%)
  starting transfers between devices  38.2 us (12%)
  matrix products  24 us (8%)
  other arithmetic  12.1 us (4%)
  between operations  8.86 us (3%)
  local copies, waits for them, and re-layouts  6.48 us (2%)
    ppermute x9, waiting for transfers between devices, extended(): lax.ppermute(lax.slice_in_dim(block, 0, width, axis=dim), axis, backward)  89.4 us
    psum x2, blocking collectives, handle_the_steps_all(): before = lax.psum(arr_in, device_axis)  67 us
    psum x1, blocking collectives, shards(): lax.psum((0.5 * jnp.dot(basis, basis.T, precision=hi), 0.5 * jnp.dot(basi...  39.9 us
    ppermute x9, starting transfers between devices, extended(): lax.ppermute(lax.slice_in_dim(block, 0, width, axis=dim), axis, backward)  25.8 us
    psum x2, blocking collectives, handle_the_steps_all(): return lax.psum(before, axis_name=named_axis)  11.1 us
    ppermute x9, waiting for transfers between devices, extended(): lax.ppermute(lax.slice_in_dim(block, block.shape[dim] - width, None, axis...  9.64 us
    dot_general x2, matrix products, shards(): local = jnp.dot(stiff, direction, precision=hi)  9.54 us
    dot_general x1, matrix products, shards(): lax.dot_general(flat, flat, (((0,), (0,)), ((), ())), preferred_element_t...  7.6 us
  transfers between devices with their start and end apart: 19, of which 17 were waited for; matrix products, arithmetic and copies ran while one was open for 1% of the time, Pallas kernels for 0%

profile of v1, /device:TPU:12, one launch (start us, length us, event | category | flops | bytes accessed | tf_op | source)
XLA Modules:
  0.0 306.6 jit_solution(18298964921047866385)
XLA Ops:
  0.6 0.7 iota_compare_fusion.1
  1.4 2.5 broadcast_select_fusion
  3.9 3.0 fusion
  6.8 4.3 %copy.15 = bf16[16,128,1024]{2,1,0:T(8,128)(2,1)} copy(bf16[16,128,1024]{2,0,1:T(8,128)(2,1)S(1)} %fusion) | data formatting | bytes 8388608 | tf_op jit(solution)/shard_map/dot_general | solution.py:50
  11.1 6.4 %all-to-all-start = ((bf16[16,128,1024]{2,1,0:T(8,128)(2,1)}), bf16[16,128,1024]{2,1,0:T(8,128)(2,1)}, u32[]{:S(2)}, u32[]{:S(2)}) async-start(bf16[16,128,1024]{2,1,0:T(8,128)(2,1)} %copy.15), calls=%async_computation | async-start | bytes 8388608 | tf_op jit(solution)/shard_map/all_to_all | solution.py:54
  17.6 1.6 collective-permute-start
  19.1 0.5 collective-permute-start.1
  19.7 1.9 collective-permute-done
  21.5 1.5 collective-permute-done.1
  23.6 16.4 %collective-permute-done.2 = f32[3,1,1,7,1024]{4,3,2,1,0:T(8,128)S(1)} collective-permute-done((f32[3,1,1,7,1024]{4,3,2,1,0:T(8,128)S(1)}, f32[3,1,1,7,1024]{4,3,2,1,0:T(8,128)S(1)}, u32[]{:S(2)}, u32[]{:S(2)}) %collective-permute-start.2) | collective-permute-done | bytes 86048 | tf_op jit(solution)/shard_map/ppermute | solution.py:18
  40.5 19.8 %collective-permute-start.4 = (f32[3,3,1,7,1024]{4,3,2,1,0:T(8,128)S(1)}, f32[3,3,1,7,1024]{4,3,2,1,0:T(8,128)S(1)}, u32[]{:S(2)}, u32[]{:S(2)}) collective-permute-start(f32[3,3,1,7,1024]{4,3,2,1,0:T(8,128)S(1)} %pad_maximum_fusion), channel_id=1, source_target_pairs={{1,0},{2,1},{3,2},{0,3},{5,4},{6,5},{7,6},{4,7},{9,8},{10,9},{11,1... | collective-permute-start | bytes 774152 | tf_op jit(solution)/shard_map/ppermute | solution.py:18
  60.3 62.5 %collective-permute-done.4 = f32[3,3,1,7,1024]{4,3,2,1,0:T(8,128)S(1)} collective-permute-done((f32[3,3,1,7,1024]{4,3,2,1,0:T(8,128)S(1)}, f32[3,3,1,7,1024]{4,3,2,1,0:T(8,128)S(1)}, u32[]{:S(2)}, u32[]{:S(2)}) %collective-permute-start.4) | collective-permute-done | bytes 258080 | tf_op jit(solution)/shard_map/ppermute | solution.py:18
  122.8 0.6 multiply_reduce_fusion.3
  124.4 39.9 %all-reduce = (f32[6,6]{1,0:T(8,128)S(1)}, f32[6]{0:T(128)S(1)}, f32[]{:T(128)}) all-reduce(f32[6,6]{1,0:T(8,128)S(1)} %convolution_multiply_fusion, f32[6]{0:T(128)S(1)} %fusion.13, f32[]{:T(128)S(6)} %mul.83), channel_id=1, replica_groups=mesh['gx'=2,'gy'=4,'gz'=4] {'gx','gy','gz'}, use_global_device_ids=true, to_apply=%region_3.4 | all-reduce | flops 43 | bytes 344 | tf_op jit(solution)/shard_map/psum | solution.py:64
  164.9 0.6 compare_reduce_fusion
  165.6 0.6 fusion.30
  166.8 0.8 fusion.48
  167.8 7.6 %fusion.53 = f32[1024,1024,1]{1,0,2:T(8,128)S(1)} fusion(bf16[16,128,1024]{2,1,0:T(8,128)(2,1)} %all-to-all-done), kind=kOutput, calls=%fused_computation.129 | convolution fusion | flops 4294967296 | bytes 8388608 | tf_op jit(solution)/shard_map/dot_general | solution.py:56
  175.4 1.9 copy-done
  177.3 3.7 %fusion.4 = f32[1,1024]{1,0:T(1,128)S(1)} fusion(f32[1024,1]{0,1:T(1,128)S(1)} %bitcast.222, f32[1024,1024,1]{1,0,2:T(8,128)S(1)} %fusion.53, f32[1024]{0:T(1024)S(1)} %bitcast.240), kind=kOutput, calls=%fused_computation.7 | convolution fusion | flops 15728640 | bytes 4206592 | tf_op jit(solution)/shard_map/dot_general | solution.py:79
  181.0 0.6 collective-permute-start.6
  181.6 1.5 collective-permute-start.7
  183.1 1.6 collective-permute-done.6
  184.6 0.6 collective-permute-done.7
  185.8 0.9 collective-permute-done.8
  186.7 1.8 collective-permute-done.9
  188.5 2.1 collective-permute-start.10
  190.7 1.8 collective-permute-done.10
  192.5 2.1 collective-permute-done.11
  194.6 0.6 multiply_reduce_fusion.1
  198.0 33.8 %all-reduce.2 = (f32[]{:T(128)}, f32[]{:T(128)}, f32[6]{0:T(128)S(1)}) all-reduce(f32[]{:T(128)S(6)} %mul.88, f32[]{:T(128)S(6)} %mul.95, f32[6]{0:T(128)S(1)} %fusion.12), channel_id=1, replica_groups=mesh['gx'=2,'gy'=4,'gz'=4] {'gy','gz'}, use_global_device_ids=true, to_apply=%region_7.9 | all-reduce | flops 8 | bytes 64 | tf_op jit(solution)/shard_map/psum | solution.py:84
  231.8 5.5 %all-reduce.4 = (f32[]{:T(128)}, f32[]{:T(128)}, f32[6]{0:T(128)S(1)}) all-reduce(f32[]{:T(128)} %get-tuple-element.11, f32[]{:T(128)} %get-tuple-element.12, f32[6]{0:T(128)S(1)} %get-tuple-element.13), channel_id=1, replica_groups=mesh['gx'=2,'gy'=4,'gz'=4] {'gx'}, use_global_device_ids=true, to_apply=%region_8.10 | all-reduce | flops 8 | bytes 64 | tf_op jit(solution)/shard_map/psum | solution.py:85
  237.5 0.7 fusion.45
  238.2 0.7 fusion.15
  242.4 5.9 %fusion.3 = f32[1,1024]{1,0:T(1,128)S(1)} fusion(f32[1024,1]{0,1:T(1,128)S(1)} %bitcast.223, f32[1024,1024,1]{1,0,2:T(8,128)} %copy-done, f32[1024]{0:T(1024)S(1)} %bitcast.241), kind=kOutput, calls=%fused_computation.6 | convolution fusion | flops 15728640 | bytes 4206592 | tf_op jit(solution)/shard_map/dot_general | solution.py:79
  248.3 1.5 collective-permute-start.12
  249.8 0.6 collective-permute-start.13
  250.3 1.6 collective-permute-done.12
  251.9 1.5 collective-permute-done.13
  254.0 0.9 collective-permute-done.14
  254.8 1.8 collective-permute-done.15
  256.7 2.0 collective-permute-start.17
  258.8 1.9 collective-permute-done.16
  260.8 0.6 multiply_reduce_fusion
  262.2 4.0 %fusion.6 = bf16[1,1024,1024]{2,1,0:T(8,128)(2,1)} fusion(f32[1024,1024,1]{1,0,2:T(8,128)} %copy-done, f32[1024]{0:T(1024)S(1)} %bitcast.242), kind=kLoop, calls=%fused_computation.9 | loop fusion | flops 4194304 | bytes 6295552 | tf_op jit(solution)/shard_map/broadcast_in_dim | solution.py:58
  266.1 33.2 %all-reduce.1 = (f32[]{:T(128)}, f32[6]{0:T(128)S(1)}) all-reduce(f32[]{:T(128)S(6)} %mul.103, f32[6]{0:T(128)S(1)} %fusion.11), channel_id=1, replica_groups=mesh['gx'=2,'gy'=4,'gz'=4] {'gy','gz'}, use_global_device_ids=true, to_apply=%region_15.17 | all-reduce | flops 7 | bytes 56 | tf_op jit(solution)/shard_map/psum | solution.py:84
  299.3 5.5 %all-reduce.3 = (f32[]{:T(128)}, f32[6]{0:T(128)S(1)}) all-reduce(f32[]{:T(128)} %get-tuple-element.9, f32[6]{0:T(128)S(1)} %get-tuple-element.10), channel_id=1, replica_groups=mesh['gx'=2,'gy'=4,'gz'=4] {'gx'}, use_global_device_ids=true, to_apply=%region_16.18 | all-reduce | flops 7 | bytes 56 | tf_op jit(solution)/shard_map/psum | solution.py:85
  306.0 0.6 multiply_subtract_fusion
  (86 shorter events, 5.4 us)
Async XLA Ops:
  1.4 2.5 copy-start.4
  11.1 6.4 %copy-start.2 = (f32[1,6,1024]{2,0,1:T(1,128)S(1)}, f32[1,6,1024]{2,0,1:T(1,128)}, u32[]{:S(2)}) copy-start(f32[1,6,1024]{2,0,1:T(1,128)} %param.13) | copy-start | bytes 73732
  11.1 6.4 %copy-start.3 = (f32[1,1024]{1,0:T(1,128)S(1)}, f32[1,1024]{1,0:T(1,128)}, u32[]{:S(2)}) copy-start(f32[1,1024]{1,0:T(1,128)} %param.12) | copy-start | bytes 12292
  11.1 156.6 %all-to-all-start = ((bf16[16,128,1024]{2,1,0:T(8,128)(2,1)}), bf16[16,128,1024]{2,1,0:T(8,128)(2,1)}, u32[]{:S(2)}, u32[]{:S(2)}) async-start(bf16[16,128,1024]{2,1,0:T(8,128)(2,1)} %copy.15), calls=%async_computation | async-start | bytes 8388608 | tf_op jit(solution)/shard_map/all_to_all | solution.py:54
  17.6 4.0 %collective-permute-start = (f32[1,1,1,7,1024]{4,3,2,1,0:T(8,128)S(1)}, f32[1,1,1,7,1024]{4,3,2,1,0:T(8,128)S(1)}, u32[]{:S(2)}, u32[]{:S(2)}) collective-permute-start(f32[1,1,1,7,1024]{4,3,2,1,0:T(8,128)S(1)} %fusion.17), channel_id=1, source_target_pairs={{16,0},{0,16},{17,1},{1,17},{18,2},{2,18},{19,3},{3,19},{20,4},{4,... | collective-permute-start | bytes 86024 | tf_op jit(solution)/shard_map/ppermute | solution.py:18
  19.1 3.9 %collective-permute-start.1 = (f32[1,1,1,7,1024]{4,3,2,1,0:T(8,128)S(1)}, f32[1,1,1,7,1024]{4,3,2,1,0:T(8,128)S(1)}, u32[]{:S(2)}, u32[]{:S(2)}) collective-permute-start(f32[1,1,1,7,1024]{4,3,2,1,0:T(8,128)S(1)} %fusion.17), channel_id=1, source_target_pairs={{0,16},{16,0},{1,17},{17,1},{2,18},{18,2},{3,19},{19,3},{4,20},{20... | collective-permute-start | bytes 86024 | tf_op jit(solution)/shard_map/ppermute | solution.py:15
  23.1 16.9 %collective-permute-start.2 = (f32[3,1,1,7,1024]{4,3,2,1,0:T(8,128)S(1)}, f32[3,1,1,7,1024]{4,3,2,1,0:T(8,128)S(1)}, u32[]{:S(2)}, u32[]{:S(2)}) collective-permute-start(f32[3,1,1,7,1024]{4,3,2,1,0:T(8,128)S(1)} %pad_maximum_fusion.1), channel_id=1, source_target_pairs={{4,0},{8,4},{12,8},{0,12},{5,1},{9,5},{13,9},{1,13},{6,2},{10,6},{... | collective-permute-start | bytes 258056 | tf_op jit(solution)/shard_map/ppermute | solution.py:18
  23.1 17.3 %collective-permute-start.3 = (f32[3,1,1,7,1024]{4,3,2,1,0:T(8,128)S(1)}, f32[3,1,1,7,1024]{4,3,2,1,0:T(8,128)S(1)}, u32[]{:S(2)}, u32[]{:S(2)}) collective-permute-start(f32[3,1,1,7,1024]{4,3,2,1,0:T(8,128)S(1)} %pad_maximum_fusion.1), channel_id=1, source_target_pairs={{0,4},{4,8},{8,12},{12,0},{1,5},{5,9},{9,13},{13,1},{2,6},{6,10},{... | collective-permute-start | bytes 258056 | tf_op jit(solution)/shard_map/ppermute | solution.py:15
  40.5 82.2 %collective-permute-start.4 = (f32[3,3,1,7,1024]{4,3,2,1,0:T(8,128)S(1)}, f32[3,3,1,7,1024]{4,3,2,1,0:T(8,128)S(1)}, u32[]{:S(2)}, u32[]{:S(2)}) collective-permute-start(f32[3,3,1,7,1024]{4,3,2,1,0:T(8,128)S(1)} %pad_maximum_fusion), channel_id=1, source_target_pairs={{1,0},{2,1},{3,2},{0,3},{5,4},{6,5},{7,6},{4,7},{9,8},{10,9},{11,1... | collective-permute-start | bytes 774152 | tf_op jit(solution)/shard_map/ppermute | solution.py:18
  60.2 62.5 %collective-permute-start.5 = (f32[3,3,1,7,1024]{4,3,2,1,0:T(8,128)S(1)}, f32[3,3,1,7,1024]{4,3,2,1,0:T(8,128)S(1)}, u32[]{:S(2)}, u32[]{:S(2)}) collective-permute-start(f32[3,3,1,7,1024]{4,3,2,1,0:T(8,128)S(1)} %pad_maximum_fusion), channel_id=1, source_target_pairs={{0,1},{1,2},{2,3},{3,0},{4,5},{5,6},{6,7},{7,4},{8,9},{9,10},{10,1... | collective-permute-start | bytes 774152 | tf_op jit(solution)/shard_map/ppermute | solution.py:15
  167.7 9.6 %copy-start.1 = (f32[1,1024]{1,0:T(1,128)S(1)}, f32[1,1024]{1,0:T(1,128)}, u32[]{:S(2)}) copy-start(f32[1,1024]{1,0:T(1,128)} %param.11) | copy-start | bytes 12292
  175.4 1.9 copy-start
  181.0 3.6 %collective-permute-start.6 = (f32[1,1,1,1,1024]{4,3,2,1,0:T(1,128)S(1)}, f32[1,1,1,1,1024]{4,3,2,1,0:T(1,128)S(1)}, u32[]{:S(2)}, u32[]{:S(2)}) collective-permute-start(f32[1,1,1,1,1024]{4,3,2,1,0:T(1,128)S(1)} %bitcast.224), channel_id=1, source_target_pairs={{16,0},{0,16},{17,1},{1,17},{18,2},{2,18},{19,3},{3,19},{20,4},{4,... | collective-permute-start | bytes 12296 | tf_op jit(solution)/shard_map/ppermute | solution.py:18
  181.6 3.6 %collective-permute-start.7 = (f32[1,1,1,1,1024]{4,3,2,1,0:T(1,128)S(1)}, f32[1,1,1,1,1024]{4,3,2,1,0:T(1,128)S(1)}, u32[]{:S(2)}, u32[]{:S(2)}) collective-permute-start(f32[1,1,1,1,1024]{4,3,2,1,0:T(1,128)S(1)} %bitcast.225), channel_id=1, source_target_pairs={{0,16},{16,0},{1,17},{17,1},{2,18},{18,2},{3,19},{19,3},{4,20},{20... | collective-permute-start | bytes 12296 | tf_op jit(solution)/shard_map/ppermute | solution.py:15
  185.2 1.5 collective-permute-start.8
  185.3 3.2 %collective-permute-start.9 = (f32[3,1,1,1,1024]{4,3,2,1,0:T(1,128)S(1)}, f32[3,1,1,1,1024]{4,3,2,1,0:T(1,128)S(1)}, u32[]{:S(2)}, u32[]{:S(2)}) collective-permute-start(f32[3,1,1,1,1024]{4,3,2,1,0:T(1,128)S(1)} %pad_maximum_fusion.5), channel_id=1, source_target_pairs={{0,4},{4,8},{8,12},{12,0},{1,5},{5,9},{9,13},{13,1},{2,6},{6,10},{... | collective-permute-start | bytes 36872 | tf_op jit(solution)/shard_map/ppermute | solution.py:15
  188.5 4.0 %collective-permute-start.10 = (f32[3,3,1,1,1024]{4,3,2,1,0:T(1,128)S(1)}, f32[3,3,1,1,1024]{4,3,2,1,0:T(1,128)S(1)}, u32[]{:S(2)}, u32[]{:S(2)}) collective-permute-start(f32[3,3,1,1,1024]{4,3,2,1,0:T(1,128)S(1)} %pad_maximum_fusion.2), channel_id=1, source_target_pairs={{1,0},{2,1},{3,2},{0,3},{5,4},{6,5},{7,6},{4,7},{9,8},{10,9},{11,1... | collective-permute-start | bytes 110600 | tf_op jit(solution)/shard_map/ppermute | solution.py:18
  190.6 4.0 %collective-permute-start.11 = (f32[3,3,1,1,1024]{4,3,2,1,0:T(1,128)S(1)}, f32[3,3,1,1,1024]{4,3,2,1,0:T(1,128)S(1)}, u32[]{:S(2)}, u32[]{:S(2)}) collective-permute-start(f32[3,3,1,1,1024]{4,3,2,1,0:T(1,128)S(1)} %pad_maximum_fusion.2), channel_id=1, source_target_pairs={{0,1},{1,2},{2,3},{3,0},{4,5},{5,6},{6,7},{7,4},{8,9},{9,10},{10,1... | collective-permute-start | bytes 110600 | tf_op jit(solution)/shard_map/ppermute | solution.py:15
  248.3 3.6 %collective-permute-start.12 = (f32[1,1,1,1,1024]{4,3,2,1,0:T(1,128)S(1)}, f32[1,1,1,1,1024]{4,3,2,1,0:T(1,128)S(1)}, u32[]{:S(2)}, u32[]{:S(2)}) collective-permute-start(f32[1,1,1,1,1024]{4,3,2,1,0:T(1,128)S(1)} %bitcast.229), channel_id=1, source_target_pairs={{16,0},{0,16},{17,1},{1,17},{18,2},{2,18},{19,3},{3,19},{20,4},{4,... | collective-permute-start | bytes 12296 | tf_op jit(solution)/shard_map/ppermute | solution.py:18
  249.8 3.6 %collective-permute-start.13 = (f32[1,1,1,1,1024]{4,3,2,1,0:T(1,128)S(1)}, f32[1,1,1,1,1024]{4,3,2,1,0:T(1,128)S(1)}, u32[]{:S(2)}, u32[]{:S(2)}) collective-permute-start(f32[1,1,1,1,1024]{4,3,2,1,0:T(1,128)S(1)} %bitcast.230), channel_id=1, source_target_pairs={{0,16},{16,0},{1,17},{17,1},{2,18},{18,2},{3,19},{19,3},{4,20},{20... | collective-permute-start | bytes 12296 | tf_op jit(solution)/shard_map/ppermute | solution.py:15
  253.4 1.5 collective-permute-start.14
  253.4 3.2 %collective-permute-start.15 = (f32[3,1,1,1,1024]{4,3,2,1,0:T(1,128)S(1)}, f32[3,1,1,1,1024]{4,3,2,1,0:T(1,128)S(1)}, u32[]{:S(2)}, u32[]{:S(2)}) collective-permute-start(f32[3,1,1,1,1024]{4,3,2,1,0:T(1,128)S(1)} %pad_maximum_fusion.6), channel_id=1, source_target_pairs={{0,4},{4,8},{8,12},{12,0},{1,5},{5,9},{9,13},{13,1},{2,6},{6,10},{... | collective-permute-start | bytes 36872 | tf_op jit(solution)/shard_map/ppermute | solution.py:15
  256.7 4.0 %collective-permute-start.16 = (f32[3,3,1,1,1024]{4,3,2,1,0:T(1,128)S(1)}, f32[3,3,1,1,1024]{4,3,2,1,0:T(1,128)S(1)}, u32[]{:S(2)}, u32[]{:S(2)}) collective-permute-start(f32[3,3,1,1,1024]{4,3,2,1,0:T(1,128)S(1)} %pad_maximum_fusion.3), channel_id=1, source_target_pairs={{1,0},{2,1},{3,2},{0,3},{5,4},{6,5},{7,6},{4,7},{9,8},{10,9},{11,1... | collective-permute-start | bytes 110600 | tf_op jit(solution)/shard_map/ppermute | solution.py:18
  256.7 4.0 %collective-permute-start.17 = (f32[3,3,1,1,1024]{4,3,2,1,0:T(1,128)S(1)}, f32[3,3,1,1,1024]{4,3,2,1,0:T(1,128)S(1)}, u32[]{:S(2)}, u32[]{:S(2)}) collective-permute-start(f32[3,3,1,1,1024]{4,3,2,1,0:T(1,128)S(1)} %pad_maximum_fusion.3), channel_id=1, source_target_pairs={{0,1},{1,2},{2,3},{3,0},{4,5},{5,6},{6,7},{7,4},{8,9},{9,10},{10,1... | collective-permute-start | bytes 110600 | tf_op jit(solution)/shard_map/ppermute | solution.py:15
